TPU v7x, 32 devices: a whole 2x2x4 slice. The times are simulated.
32 devices in a mesh: tok: 8 (over z, y), voc: 4 (over x, core).
Axes of the slice: x: 2, y: 2, z: 4, core: 2. Of those that a mesh axis runs over, the one named last changes fastest.
Arguments:
- hidden: bfloat16 [96, 4096], P(('tok', 'voc'))
- head_weight: bfloat16 [4096, 16032], P(None, ('tok', 'voc'))
- actions: int32 [96], P(('tok', 'voc')), may hold values from 0 to 16031
- old_logp: bfloat16 [96], P(('tok', 'voc')), may hold values from -80 to 1
- advantage: bfloat16 [96], P(('tok', 'voc')), may hold values from -4 to 4
- loss_mask: int32 [96], P(('tok', 'voc')), may hold values 0 or 1
Outputs:
- grad_weight: bfloat16 [4096, 16032], P(None, ('tok', 'voc'))
- grad_hidden: float32 [96, 4096], P(('tok', 'voc'))
All inputs are finite; a program needn't handle non-finite values. No bound on the sum of `loss_mask` on one device may be relied on, other than what follows from the above.
Results may differ from a plain program's by a relative error of at most 0.0047.
Values may be sent and summed in bfloat16 or wider, within the bound.
A program may use at most 128 MiB of HBM per device.

v0:
```python
import jax
import jax.numpy as jnp
from jax import lax
from jax.sharding import PartitionSpec as P


def per_device(hidden, head_weight, actions, old_logp, advantage, loss_mask):
    hidden_all, old_all, advant_all = (
        lax.all_gather(hidden, ("tok", "voc"), axis=0, tiled=True),
        lax.all_gather(old_logp, ("tok", "voc"), axis=0, tiled=True),
        lax.all_gather(advantage, ("tok", "voc"), axis=0, tiled=True),
    )
    action_all, mask_all = (
        lax.all_gather(actions, ("tok", "voc"), axis=0, tiled=True),
        lax.all_gather(loss_mask, ("tok", "voc"), axis=0, tiled=True),
    )
    width = head_weight.shape[1]
    logits = jnp.dot(hidden_all, head_weight, preferred_element_type=jnp.float32)
    first_col = lax.axis_index(("tok", "voc")) * width
    columns = first_col + lax.broadcasted_iota(jnp.int32, logits.shape, 1)
    matches = columns == action_all[:, None]
    target_part = jnp.sum(jnp.where(matches, logits, 0.0), axis=1)
    top = lax.pmax(jnp.max(logits, axis=1), ("tok", "voc"))
    shifted = jnp.exp(logits - top[:, None])
    sumexp, moment, target = lax.psum(
        (jnp.sum(shifted, axis=1), jnp.sum(shifted * logits, axis=1), target_part), ("tok", "voc")
    )
    lse = top + jnp.log(sumexp)
    mean_logit = moment / sumexp
    advant = advant_all.astype(jnp.float32)
    ratio = jnp.exp(target - lse - old_all.astype(jnp.float32))
    clipped = (advant > 0.0) & (ratio > 1.2) | (advant < 0.0) & (ratio < 0.8)
    active = jnp.where(clipped, 0.0, 1.0).astype(jnp.float32)
    weights = mask_all.astype(jnp.float32)
    policy = -advant * ratio * active * weights
    probability = jnp.exp(logits - lse[:, None])
    onehot = matches.astype(jnp.float32)
    dlogits = policy[:, None] * (onehot - probability) + 0.05 * weights[:, None] * probability * (
        logits - mean_logit[:, None]
    )
    dlogits = dlogits.astype(jnp.bfloat16)
    partial_rows = lax.psum_scatter(
        lax.dot_general(
            dlogits, head_weight, (((1,), (1,)), ((), ())), preferred_element_type=jnp.float32
        ),
        "tok",
        scatter_dimension=0,
        tiled=True,
    )
    grad_hidden = lax.psum_scatter(partial_rows, "voc", scatter_dimension=0, tiled=True)
    grad_weight = lax.dot_general(
        hidden_all, dlogits, (((0,), (0,)), ((), ())), preferred_element_type=jnp.float32
    ).astype(jnp.bfloat16)
    return (grad_weight, grad_hidden)


def solution(mesh):
    placed = (
        P(("tok", "voc"), None),
        P(None, ("tok", "voc")),
        P(("tok", "voc")),
        P(("tok", "voc")),
        P(("tok", "voc")),
        P(("tok", "voc")),
    )
    return jax.shard_map(
        per_device,
        mesh=mesh,
        in_specs=placed,
        out_specs=(P(None, ("tok", "voc")), P(("tok", "voc"), None)),
        check_vma=False,
    )
```

profile of v0, /device:TPU:0, one launch (start us, length us, event | category | flops | bytes accessed | tf_op | source)
XLA Modules:
  0.0 323.1 jit_solution(7266715647205631639)
XLA Ops:
  7.2 0.0 copy-start.1
  7.2 0.0 copy-start.2
  7.2 0.0 copy-start.3
  7.2 0.0 copy-start.4
  7.2 0.0 all-reduce.12.cloned.1.call-start
  7.3 46.5 %all-gather = bf16[32,3,4096]{2,1,0:T(4,128)(2,1)S(1)} all-gather(bf16[1,3,4096]{2,1,0:T(4,128)(2,1)} %bitcast.11), channel_id=1, replica_groups=mesh['tok'=8,'voc'=4] {'tok','voc'}, dimensions={0}, use_global_device_ids=true | all-gather | bytes 811008 | tf_op jit(solution)/shard_map/all_gather | solution.py:9
  53.7 0.7 reshape.20
  54.4 3.6 %fusion.12 = (f32[96]{0:T(128)S(1)}, f32[96,501]{1,0:T(8,128)S(1)}) fusion(bf16[96,4096]{1,0:T(8,128)(2,1)S(1)} %reshape.20, bf16[4096,501]{0,1:T(8,128)(2,1)} %param.7), kind=kOutput, calls=%fused_computation.21 | convolution fusion | flops 394050432 | bytes 5083392 | tf_op jit(solution)/shard_map/dot_general | solution.py:18
  58.0 36.9 %pmax.7 = f32[96]{0:T(128)S(1)} all-reduce(f32[96]{0:T(128)S(1)} %get-tuple-element.16), channel_id=1, replica_groups=mesh['tok'=8,'voc'=4] {'tok','voc'}, use_global_device_ids=true, to_apply=%region_3.4 | all-reduce | flops 96 | bytes 768 | tf_op jit(solution)/shard_map/pmax | solution.py:23
  94.9 0.0 copy-done.1
  94.9 0.2 dynamic-update-slice.2
  95.1 0.0 copy-done.2
  95.1 0.2 dynamic-update-slice
  95.4 41.1 %all-reduce.9 = (bf16[96]{0:T(256)(128)(2,1)S(1)}, bf16[96]{0:T(256)(128)(2,1)S(1)}) all-reduce(bf16[96]{0:T(256)(128)(2,1)S(1)} %dynamic-update-slice.2, bf16[96]{0:T(256)(128)(2,1)S(1)} %dynamic-update-slice), channel_id=1, replica_groups=mesh['tok'=8,'voc'=4] {'tok','voc'}, use_global_device_ids=true, to_apply=%add.2 | all-reduce | flops 192 | bytes 768
  136.5 0.0 copy-done.3
  136.5 0.2 dynamic-update-slice.1
  136.7 0.0 copy-done.4
  136.7 0.2 dynamic-update-slice.3
  137.0 39.5 %all-reduce.7 = (s32[96]{0:T(128)S(1)}, s32[96]{0:T(128)S(1)}) all-reduce(s32[96]{0:T(128)S(1)} %dynamic-update-slice.1, s32[96]{0:T(128)S(1)} %dynamic-update-slice.3), channel_id=1, replica_groups=mesh['tok'=8,'voc'=4] {'tok','voc'}, use_global_device_ids=true, to_apply=%add.1 | all-reduce | flops 192 | bytes 1536
  176.4 0.2 fusion.7
  176.7 40.5 %all-reduce.8 = (f32[96]{0:T(128)S(1)}, f32[96]{0:T(128)S(1)}, f32[96]{0:T(128)S(1)}) all-reduce(f32[96]{0:T(128)S(1)} %get-tuple-element.3, f32[96]{0:T(128)S(1)} %get-tuple-element.2, f32[96]{0:T(128)S(1)} %get-tuple-element.4), channel_id=1, replica_groups=mesh['tok'=8,'voc'=4] {'tok','voc'}, use_global_device_ids=true, to_apply=%region_7.8 | all-reduce | flops 288 | bytes 2304 | tf_op jit(solution)/shard_map/psum | solution.py:25
  217.1 0.0 copy-start
  217.2 3.2 fusion.9
  220.3 46.1 %fusion = f32[16,4096]{1,0:T(8,128)S(1)} fusion(f32[96,4096]{1,0:T(8,128)S(1)} %fusion.9), kind=kCustom, calls=%all-reduce-scatter | all-reduce-scatter fusion | flops 524289 | bytes 1835520
  266.5 4.3 %collective-permute-start = (f32[16,4096]{1,0:T(8,128)S(1)}, f32[16,4096]{1,0:T(8,128)S(1)}, u32[]{:S(2)}, u32[]{:S(2)}) collective-permute-start(f32[16,4096]{1,0:T(8,128)S(1)} %fusion), channel_id=1, source_target_pairs={{0,4},{4,8},{8,12},{12,16},{16,20},{20,24},{24,28},{1,5},{5,9},{9,... | collective-permute-start | bytes 786440
  270.8 2.7 collective-permute-start.1
  273.5 0.0 copy-done
  273.5 0.6 dynamic-slice.6
  274.7 2.6 collective-permute-done.1
  277.3 0.0 collective-permute-done
  277.3 0.6 concatenate
  278.0 0.0 copy-start.5
  278.0 0.7 constant_dynamic-slice_fusion
  278.7 0.0 all-reduce.12.cloned.1.call-update
  278.7 3.4 %fusion.1 = bf16[4096,501]{0,1:T(8,128)(2,1)} fusion(bf16[96,4096]{1,0:T(8,128)(2,1)S(1)} %reshape.20, f32[96,501]{1,0:T(8,128)S(1)} %get-tuple-element.17, f32[96]{0:T(128)S(1)} %get-tuple-element.14, f32[96]{0:T(128)S(1)} %get-tuple-element.15, f32[96]{0:T(128)S(1)} %get-tuple-element.13, f32[96]{0:T(128)S(1)} %get-tuple-element.12, ...), kind=kOutput, calls=%fused_computation.1 | convolution fusion | flops 396535488 | bytes 5086932 | tf_op jit(solution)/shard_map/dot_general | solution.py:51
  282.1 0.0 copy-done.5
  282.1 0.6 dynamic-slice.2
  283.4 31.4 %all-reduce.12.cloned.1.call-done = f32[12,4096]{1,0:T(8,128)} async-done(((f32[12,4096]{1,0:T(8,128)}), f32[12,4096]{1,0:T(8,128)}) %all-reduce.12.cloned.1.call-update) | async-done | bytes 196624
  314.7 1.6 constant_dynamic-slice_fusion.1
  (7 shorter events, 0.1 us)
Async XLA Ops:
  7.2 87.7 %copy-start.1 = (bf16[3]{0:T(256)(128)(2,1)S(1)}, bf16[3]{0:T(256)(128)(2,1)}, u32[]{:S(2)}) copy-start(bf16[3]{0:T(256)(128)(2,1)} %param.9) | copy-start | bytes 22
  7.2 88.0 %copy-start.2 = (bf16[3]{0:T(256)(128)(2,1)S(1)}, bf16[3]{0:T(256)(128)(2,1)}, u32[]{:S(2)}) copy-start(bf16[3]{0:T(256)(128)(2,1)} %param.10) | copy-start | bytes 22
  7.2 129.3 %copy-start.3 = (s32[3]{0:T(128)S(1)}, s32[3]{0:T(128)}, u32[]{:S(2)}) copy-start(s32[3]{0:T(128)} %param.8) | copy-start | bytes 40
  7.2 129.5 %copy-start.4 = (s32[3]{0:T(128)S(1)}, s32[3]{0:T(128)}, u32[]{:S(2)}) copy-start(s32[3]{0:T(128)} %param.11) | copy-start | bytes 40
  7.2 307.5 %all-reduce.12.cloned.1.call-start = ((), (), s32[]{:S(2)}) async-start(), calls=%async_computation | async-start | bytes 524288
  217.1 56.3 %copy-start = (u32[32]{0:T(128)S(1)}, u32[32]{0:T(128)}, u32[]{:S(2)}) copy-start(u32[32]{0:T(128)} %constant.50) | copy-start | bytes 388
  266.5 10.9 %collective-permute-start = (f32[16,4096]{1,0:T(8,128)S(1)}, f32[16,4096]{1,0:T(8,128)S(1)}, u32[]{:S(2)}, u32[]{:S(2)}) collective-permute-start(f32[16,4096]{1,0:T(8,128)S(1)} %fusion), channel_id=1, source_target_pairs={{0,4},{4,8},{8,12},{12,16},{16,20},{20,24},{24,28},{1,5},{5,9},{9,... | collective-permute-start | bytes 786440
  270.8 6.6 %collective-permute-start.1 = (f32[12,4096]{1,0:T(8,128)S(1)}, f32[12,4096]{1,0:T(8,128)S(1)}, u32[]{:S(2)}, u32[]{:S(2)}) collective-permute-start(f32[12,4096]{1,0:T(8,128)S(1)} %slice), channel_id=1, source_target_pairs={{0,8},{4,12},{8,16},{12,20},{16,24},{20,28},{1,9},{5,13},{9,17},{1... | collective-permute-start | bytes 589832
  278.0 4.1 %copy-start.5 = (u32[32]{0:T(128)S(1)}, u32[32]{0:T(128)}, u32[]{:S(2)}) copy-start(u32[32]{0:T(128)} %constant.54) | copy-start | bytes 388
Sparse Core Ops, SparseCore 0:
  278.9 35.7 all-reduce.11
where the time goes:
time: 324 us; the launch traced here: 323 us
  blocking collectives  250 us (77%)
  waiting for transfers between devices  34 us (10%)
  between operations  15.5 us (5%)
  matrix products  10.2 us (3%)
  starting transfers between devices  7 us (2%)
  local copies, waits for them, and re-layouts  5.77 us (2%)
    unnamed x3, blocking collectives  127 us
    all_gather x1, blocking collectives, per_device(): lax.all_gather(hidden, ('tok', 'voc'), axis=0, tiled=True)  46.5 us
    psum x1, blocking collectives, per_device(): lax.psum((jnp.sum(shifted, axis=1), jnp.sum(shifted * logits, axis=1), ta...  40.5 us
    pmax x1, blocking collectives, per_device(): top = lax.pmax(jnp.max(logits, axis=1), ('tok', 'voc'))  36.9 us
    unnamed x4, waiting for transfers between devices  34 us
    unnamed x3, starting transfers between devices  7 us
  transfers between devices with their start and end apart: 3, of which 2 were waited for; matrix products, arithmetic and copies ran while one was open for 1% of the time, Pallas kernels for 0%

commit v1 on v0

--- a/solution.py
+++ b/solution.py
@@ -2,6 +2,13 @@
 import jax.numpy as jnp
 from jax import lax
 from jax.sharding import PartitionSpec as P
+from jax.lax import psum
+
+
+def wait_the_sizes(frame, bus_axis, dev_axis):
+    heard = psum(frame, axis_name=bus_axis)
+    lower = psum(heard, axis_name=dev_axis)
+    return lower
 
 
 def per_device(hidden, head_weight, actions, old_logp, advantage, loss_mask):
@@ -22,8 +29,8 @@
     target_part = jnp.sum(jnp.where(matches, logits, 0.0), axis=1)
     top = lax.pmax(jnp.max(logits, axis=1), ("tok", "voc"))
     shifted = jnp.exp(logits - top[:, None])
-    sumexp, moment, target = lax.psum(
-        (jnp.sum(shifted, axis=1), jnp.sum(shifted * logits, axis=1), target_part), ("tok", "voc")
+    sumexp, moment, target = wait_the_sizes(
+        (jnp.sum(shifted, axis=1), jnp.sum(shifted * logits, axis=1), target_part), "voc", "tok"
     )
     lse = top + jnp.log(sumexp)
     mean_logit = moment / sumexp

time: 324 us -> 301 us (0.929)
  blocking collectives: 250 us -> 230 us
    psum x1 -> x2, blocking collectives: 40.5 us -> 26.2 us  [the longest x1 20.4 us: wait_the_sizes(): lower = psum(heard, axis_name=dev_axis)]
    unnamed x3, blocking collectives: 127 us -> 121 us
  transfers between devices with their start and end apart: 3 -> 3, of which waited for: 2 -> 2; matrix products, arithmetic and copies ran while one was open for 1% -> 2% of each run, Pallas kernels for 0% -> 0%
where the time goes in v1:
time: 301 us; the launch traced here: 300 us
  blocking collectives  230 us (76%)
  waiting for transfers between devices  31.6 us (10%)
  between operations  15.5 us (5%)
  matrix products  10.1 us (3%)
  starting transfers between devices  6.26 us (2%)
  local copies, waits for them, and re-layouts  5.76 us (2%)
    unnamed x3, blocking collectives  121 us
    all_gather x1, blocking collectives, per_device(): lax.all_gather(hidden, ('tok', 'voc'), axis=0, tiled=True)  46.5 us
    pmax x1, blocking collectives, per_device(): top = lax.pmax(jnp.max(logits, axis=1), ('tok', 'voc'))  36.8 us
    unnamed x4, waiting for transfers between devices  31.6 us
    psum x1, blocking collectives, wait_the_sizes(): lower = psum(heard, axis_name=dev_axis)  20.4 us
    unnamed x3, starting transfers between devices  6.26 us
  transfers between devices with their start and end apart: 3, of which 2 were waited for; matrix products, arithmetic and copies ran while one was open for 2% of the time, Pallas kernels for 0%

profile of v1, /device:TPU:0, one launch (start us, length us, event | category | flops | bytes accessed | tf_op | source)
XLA Modules:
  0.0 299.9 jit_solution(1283064194499250868)
XLA Ops:
  7.2 0.0 copy-start.1
  7.2 0.0 copy-start.2
  7.2 0.0 copy-start.3
  7.2 0.0 copy-start.4
  7.2 0.0 all-reduce.13.cloned.1.call-start
  7.3 46.5 %all-gather = bf16[32,3,4096]{2,1,0:T(4,128)(2,1)S(1)} all-gather(bf16[1,3,4096]{2,1,0:T(4,128)(2,1)} %bitcast.11), channel_id=1, replica_groups=mesh['tok'=8,'voc'=4] {'tok','voc'}, dimensions={0}, use_global_device_ids=true | all-gather | bytes 811008 | tf_op jit(solution)/shard_map/all_gather | solution.py:16
  53.7 0.7 reshape.20
  54.4 3.6 %fusion.12 = (f32[96]{0:T(128)S(1)}, f32[96,501]{1,0:T(8,128)S(1)}) fusion(bf16[96,4096]{1,0:T(8,128)(2,1)S(1)} %reshape.20, bf16[4096,501]{0,1:T(8,128)(2,1)} %param.7), kind=kOutput, calls=%fused_computation.21 | convolution fusion | flops 394050432 | bytes 5083392 | tf_op jit(solution)/shard_map/dot_general | solution.py:25
  58.0 36.8 %pmax.7 = f32[96]{0:T(128)S(1)} all-reduce(f32[96]{0:T(128)S(1)} %get-tuple-element.19), channel_id=1, replica_groups=mesh['tok'=8,'voc'=4] {'tok','voc'}, use_global_device_ids=true, to_apply=%region_4.5 | all-reduce | flops 96 | bytes 768 | tf_op jit(solution)/shard_map/pmax | solution.py:30
  94.9 0.0 copy-done.1
  94.9 0.2 dynamic-update-slice.2
  95.1 0.0 copy-done.2
  95.1 0.2 dynamic-update-slice
  95.3 41.1 %all-reduce.10 = (bf16[96]{0:T(256)(128)(2,1)S(1)}, bf16[96]{0:T(256)(128)(2,1)S(1)}) all-reduce(bf16[96]{0:T(256)(128)(2,1)S(1)} %dynamic-update-slice.2, bf16[96]{0:T(256)(128)(2,1)S(1)} %dynamic-update-slice), channel_id=1, replica_groups=mesh['tok'=8,'voc'=4] {'tok','voc'}, use_global_device_ids=true, to_apply=%add.2 | all-reduce | flops 192 | bytes 768
  136.5 0.0 copy-done.3
  136.5 0.2 dynamic-update-slice.1
  136.7 0.0 copy-done.4
  136.7 0.2 dynamic-update-slice.3
  136.9 39.5 %all-reduce.7 = (s32[96]{0:T(128)S(1)}, s32[96]{0:T(128)S(1)}) all-reduce(s32[96]{0:T(128)S(1)} %dynamic-update-slice.1, s32[96]{0:T(128)S(1)} %dynamic-update-slice.3), channel_id=1, replica_groups=mesh['tok'=8,'voc'=4] {'tok','voc'}, use_global_device_ids=true, to_apply=%add.1 | all-reduce | flops 192 | bytes 1536
  176.4 0.2 fusion.7
  176.6 5.8 %all-reduce.9 = (f32[96]{0:T(128)S(1)}, f32[96]{0:T(128)S(1)}, f32[96]{0:T(128)S(1)}) all-reduce(f32[96]{0:T(128)S(1)} %get-tuple-element.3, f32[96]{0:T(128)S(1)} %get-tuple-element.2, f32[96]{0:T(128)S(1)} %get-tuple-element.4), channel_id=1, replica_groups=mesh['tok'=8,'voc'=4] {'voc'}, use_global_device_ids=true, to_apply=%region_9.10 | all-reduce | flops 288 | bytes 2304 | tf_op jit(solution)/shard_map/psum | solution.py:9
  182.4 20.4 %all-reduce.8 = (f32[96]{0:T(128)S(1)}, f32[96]{0:T(128)S(1)}, f32[96]{0:T(128)S(1)}) all-reduce(f32[96]{0:T(128)S(1)} %get-tuple-element.10, f32[96]{0:T(128)S(1)} %get-tuple-element.11, f32[96]{0:T(128)S(1)} %get-tuple-element.12), channel_id=1, replica_groups=mesh['tok'=8,'voc'=4] {'tok'}, use_global_device_ids=true, to_apply=%region_10.11 | all-reduce | flops 288 | bytes 2304 | tf_op jit(solution)/shard_map/psum | solution.py:10
  202.9 0.0 copy-start
  202.9 3.2 %fusion.9 = f32[96,4096]{1,0:T(8,128)S(1)} fusion(bf16[4096,501]{0,1:T(8,128)(2,1)} %param.7, f32[96,501]{1,0:T(8,128)S(1)} %get-tuple-element.20, f32[96]{0:T(128)S(1)} %get-tuple-element.17, f32[96]{0:T(128)S(1)} %get-tuple-element.18, f32[96]{0:T(128)S(1)} %get-tuple-element.16, f32[96]{0:T(128)S(1)} %get-tuple-element.15, s32[501]{0:T(512)S(1)} %iota_add_fusion, ...), kind=kOutput, calls=%fused_computation.20 | convolution fusion | flops 394483392 | bytes 5873364 | tf_op jit(solution)/shard_map/dot_general | solution.py:50
  206.0 40.3 %fusion = f32[16,4096]{1,0:T(8,128)S(1)} fusion(f32[96,4096]{1,0:T(8,128)S(1)} %fusion.9), kind=kCustom, calls=%all-reduce-scatter | all-reduce-scatter fusion | flops 524289 | bytes 1835520
  246.4 2.8 collective-permute-start
  249.2 3.5 %collective-permute-start.1 = (f32[12,4096]{1,0:T(8,128)S(1)}, f32[12,4096]{1,0:T(8,128)S(1)}, u32[]{:S(2)}, u32[]{:S(2)}) collective-permute-start(f32[12,4096]{1,0:T(8,128)S(1)} %slice), channel_id=1, source_target_pairs={{0,8},{4,12},{8,16},{12,20},{16,24},{20,28},{1,9},{5,13},{9,17},{1... | collective-permute-start | bytes 589832
  252.6 0.0 copy-done
  252.6 0.6 dynamic-slice.6
  253.9 2.6 collective-permute-done.1
  256.5 0.0 collective-permute-done
  256.5 0.6 concatenate
  257.1 0.0 copy-start.5
  257.1 0.7 constant_dynamic-slice_fusion
  257.9 0.0 all-reduce.13.cloned.1.call-update
  257.9 3.4 %fusion.1 = bf16[4096,501]{0,1:T(8,128)(2,1)} fusion(bf16[96,4096]{1,0:T(8,128)(2,1)S(1)} %reshape.20, f32[96,501]{1,0:T(8,128)S(1)} %get-tuple-element.20, f32[96]{0:T(128)S(1)} %get-tuple-element.17, f32[96]{0:T(128)S(1)} %get-tuple-element.18, f32[96]{0:T(128)S(1)} %get-tuple-element.16, f32[96]{0:T(128)S(1)} %get-tuple-element.15, ...), kind=kOutput, calls=%fused_computation.1 | convolution fusion | flops 396535488 | bytes 5086932 | tf_op jit(solution)/shard_map/dot_general | solution.py:58
  261.3 0.0 copy-done.5
  261.3 0.6 dynamic-slice.2
  262.5 29.0 %all-reduce.13.cloned.1.call-done = f32[12,4096]{1,0:T(8,128)} async-done(((f32[12,4096]{1,0:T(8,128)}), f32[12,4096]{1,0:T(8,128)}) %all-reduce.13.cloned.1.call-update) | async-done | bytes 196624
  291.5 1.6 constant_dynamic-slice_fusion.1
  (7 shorter events, 0.1 us)
Async XLA Ops:
  7.2 87.7 %copy-start.1 = (bf16[3]{0:T(256)(128)(2,1)S(1)}, bf16[3]{0:T(256)(128)(2,1)}, u32[]{:S(2)}) copy-start(bf16[3]{0:T(256)(128)(2,1)} %param.9) | copy-start | bytes 22
  7.2 87.9 %copy-start.2 = (bf16[3]{0:T(256)(128)(2,1)S(1)}, bf16[3]{0:T(256)(128)(2,1)}, u32[]{:S(2)}) copy-start(bf16[3]{0:T(256)(128)(2,1)} %param.10) | copy-start | bytes 22
  7.2 129.3 %copy-start.3 = (s32[3]{0:T(128)S(1)}, s32[3]{0:T(128)}, u32[]{:S(2)}) copy-start(s32[3]{0:T(128)} %param.8) | copy-start | bytes 40
  7.2 129.5 %copy-start.4 = (s32[3]{0:T(128)S(1)}, s32[3]{0:T(128)}, u32[]{:S(2)}) copy-start(s32[3]{0:T(128)} %param.11) | copy-start | bytes 40
  7.2 284.3 %all-reduce.13.cloned.1.call-start = ((), (), s32[]{:S(2)}) async-start(), calls=%async_computation | async-start | bytes 524288
  202.9 49.8 %copy-start = (u32[32]{0:T(128)S(1)}, u32[32]{0:T(128)}, u32[]{:S(2)}) copy-start(u32[32]{0:T(128)} %constant.50) | copy-start | bytes 388
  246.4 10.1 %collective-permute-start = (f32[16,4096]{1,0:T(8,128)S(1)}, f32[16,4096]{1,0:T(8,128)S(1)}, u32[]{:S(2)}, u32[]{:S(2)}) collective-permute-start(f32[16,4096]{1,0:T(8,128)S(1)} %fusion), channel_id=1, source_target_pairs={{0,4},{4,8},{8,12},{12,16},{16,20},{20,24},{24,28},{1,5},{5,9},{9,... | collective-permute-start | bytes 786440
  249.2 7.3 %collective-permute-start.1 = (f32[12,4096]{1,0:T(8,128)S(1)}, f32[12,4096]{1,0:T(8,128)S(1)}, u32[]{:S(2)}, u32[]{:S(2)}) collective-permute-start(f32[12,4096]{1,0:T(8,128)S(1)} %slice), channel_id=1, source_target_pairs={{0,8},{4,12},{8,16},{12,20},{16,24},{20,28},{1,9},{5,13},{9,17},{1... | collective-permute-start | bytes 589832
  257.1 4.1 %copy-start.5 = (u32[32]{0:T(128)S(1)}, u32[32]{0:T(128)}, u32[]{:S(2)}) copy-start(u32[32]{0:T(128)} %constant.54) | copy-start | bytes 388
Sparse Core Ops, SparseCore 0:
  258.0 33.4 all-reduce.12
